TPU v7x, 256 devices: a whole 4x4x8 slice. The times are simulated.
256 devices in a mesh: dp: 64 (over x, z_lo, y, core), sub: 4 (over z_hi).
Axes of the slice: x: 4, y: 4, z: 8 (z_hi: 4, z_lo: 2; z = z_hi * 2 + z_lo), core: 2. Of those that a mesh axis runs over, the one named last changes fastest.
Arguments:
- queries: float32 [16384, 1024], P(('dp', 'sub')), may hold values from -8 to 8
- passages: float32 [16384, 1024], P(('dp', 'sub')), may hold values from -8 to 8
- positives: int32 [16384], P(('dp', 'sub')), may hold values from 0 to 16383, each once
Outputs:
- losses: float32 [16384], P(('dp', 'sub'))
- query_grads: float32 [16384, 1024], P(('dp', 'sub'))
- passage_grads: float32 [16384, 1024], P(('dp', 'sub'))
All inputs are finite; a program needn't handle non-finite values.
Results may differ from a plain program's by a relative error of at most 0.00185.
The roundings to bfloat16 on the way count: a program that leaves them out, or rounds other values in their place, can miss the bound.
Values may be sent and summed in bfloat16 or wider, within the bound.
No kernel may reach another device: no remote copies, remote signals or barrier semaphores. Data moves between devices by JAX's collectives and lax.ppermute only.
A program may use at most 128 MiB of HBM per device.

v0:
```python
import jax
import jax.numpy as jnp
from jax import lax
from jax.sharding import Mesh
from jax.sharding import PartitionSpec as P

DP = ("dp_0", "dp_1", "dp_2", "dp_3")
DP_SUB = ("dp_0", "dp_1", "dp_2", "dp_3", "sub")
logit_scale = 20.0


def laid_out(blocks, dim):
    blocks = jnp.moveaxis(blocks, 0, dim)
    lengths = blocks.shape
    return blocks.reshape(*lengths[:dim], lengths[dim] * lengths[dim + 1], *lengths[dim + 2 :])


def sent_to_all(value, axis):
    devices = lax.axis_size(axis)
    return lax.all_to_all(
        jnp.broadcast_to(value[None], (devices, *value.shape)), axis, 0, 0, tiled=True
    )


def collect(value, axis, dim):
    return laid_out(sent_to_all(value, axis), dim)


def gathered_once(value, axis):
    leaves = jax.tree.leaves(value)
    sequence = sorted(range(len(leaves)), key=lambda k: -leaves[k].size)
    width = (1, *leaves[sequence[0]].shape)[-1]
    lines = [
        jnp.pad(leaves[k].reshape(-1), (0, -leaves[k].size % width)).reshape(-1, width)
        for k in sequence
    ]
    both, at, found = (sent_to_all(jnp.concatenate(lines), axis), 0, {})
    for k, line in zip(sequence, lines):
        slab = both[:, at : at + len(line)].reshape(len(both), -1)
        found[k] = slab[:, : leaves[k].size].reshape(-1, *leaves[k].shape)
        at += len(line)
    numbers = iter(range(len(leaves)))
    return jax.tree.map(lambda _: found[next(numbers)], value)


def folded_in_pairs(pieces, combine):
    while len(jax.tree.leaves(pieces)[0]) > 1:
        pieces = jax.vmap(combine)(
            *(jax.tree.map(lambda part: part[side::2], pieces) for side in (0, 1))
        )
    return jax.tree.map(lambda part: part[0], pieces)


def joined_all(value, axis, combine):
    pieces = gathered_once(value, axis)
    return folded_in_pairs(pieces, combine)


def split_up(value, dim, devices):
    before, after = (value.shape[:dim], value.shape[dim + 1 :])
    return jnp.moveaxis(value.reshape(*before, devices, -1, *after), dim, 0)


def sum_at_owner(value, axis, dim):
    devices = lax.axis_size(axis)
    blocks = lax.all_to_all(split_up(value, dim, devices), axis, 0, 0, tiled=True)
    return jnp.sum(blocks, axis=0)


def scatter_pairs(value, chips, core, dim):
    sizes = (lax.axis_size(chips), lax.axis_size(core))
    blocks = split_up(value, dim, sizes[0] * sizes[1])
    inside = blocks.shape[1:]
    blocks = blocks.reshape(*sizes, *inside).swapaxes(0, 1).reshape(-1, *inside)
    blocks = lax.psum_scatter(blocks, core, scatter_dimension=0, tiled=True)
    return lax.psum_scatter(blocks, chips, scatter_dimension=0, tiled=True)[0]


def combine_rows(earlier, later):
    highest = jnp.maximum(earlier[0], later[0])
    exp_total = earlier[1] * jnp.exp(earlier[0] - highest) + later[1] * jnp.exp(later[0] - highest)
    return (highest, exp_total, earlier[2] + later[2])


def row_scores(query_rows, passage_rows):
    return (
        lax.dot_general(
            query_rows, passage_rows, (((1,), (1,)), ((), ())), preferred_element_type=jnp.float32
        )
        * logit_scale
    )


def local_stats(scores, onehot):
    highest = jnp.max(scores, axis=1)
    exp_total = jnp.sum(jnp.exp(scores - highest[:, None]), axis=1)
    positive_score = jnp.sum(onehot * scores, axis=1)
    return (highest, exp_total, positive_score)


def body(queries, passages, positives):
    row_count = queries.shape[0]
    groups = lax.axis_size("sub")
    member = lax.axis_index("sub")
    query_half = queries.astype(jnp.bfloat16)
    passage_half = passages.astype(jnp.bfloat16)
    query_rows, row_targets = (collect(query_half, "sub", 0), collect(positives, "sub", 0))
    width_cols = row_count * lax.axis_size(DP)
    passage_rows = lax.all_gather(passage_half, DP, axis=0, tiled=True)
    scores = row_scores(query_rows, passage_rows)
    column = jnp.arange(width_cols, dtype=jnp.int32)
    column_ids = (column // row_count * groups + member) * row_count + column % row_count
    onehot = (column_ids[None, :] == row_targets[:, None]).astype(jnp.float32)
    highest, exp_total, positive_score = local_stats(scores, onehot)
    highest, exp_total, positive_score = joined_all(
        (highest, exp_total, positive_score), "sub", combine_rows
    )
    log_norm = highest + jnp.log(exp_total)
    losses = lax.dynamic_slice_in_dim(log_norm - positive_score, member * row_count, row_count)
    weights = ((jnp.exp(scores - log_norm[:, None]) - onehot) * logit_scale).astype(jnp.bfloat16)
    query_terms = jnp.dot(weights, passage_rows, preferred_element_type=jnp.float32)
    query_grads = sum_at_owner(query_terms, "sub", 0)
    passage_grads = scatter_pairs(
        lax.dot_general(
            weights, query_rows, (((0,), (0,)), ((), ())), preferred_element_type=jnp.float32
        ),
        ("dp_0", "dp_1", "dp_2"),
        "dp_3",
        0,
    )
    return (losses, query_grads, passage_grads)


def solution(mesh):
    torus = Mesh(
        mesh.devices.reshape(4, 2, 4, 2, mesh.shape["sub"]), ("dp_0", "dp_1", "dp_2", "dp_3", "sub")
    )
    placed = (P(DP_SUB, None), P(DP_SUB, None), P(DP_SUB))
    return jax.shard_map(
        body,
        mesh=torus,
        in_specs=placed,
        out_specs=(P(DP_SUB), P(DP_SUB, None), P(DP_SUB, None)),
        check_vma=False,
    )
```

profile of v0, /device:TPU:64, one launch (start us, length us, event | category | flops | bytes accessed | tf_op | source)
XLA Modules:
  0.0 401.1 jit_solution(4751008625709761402)
XLA Ops:
  7.2 0.0 all-gather.2.cloned.1.call-start
  7.2 1.6 convert_element_type.19
  8.8 0.0 all-gather.2.cloned.1.call-update
  8.9 1.2 broadcast_in_dim.7
  10.1 8.1 %all-to-all-start.1 = ((s32[4,1,64]{2,1,0:T(1,128)}), s32[4,1,64]{2,1,0:T(1,128)S(1)}, u32[]{:S(2)}, u32[]{:S(2)}) async-start(s32[4,1,64]{2,1,0:T(1,128)} %broadcast_in_dim.7), calls=%async_computation.1 | async-start | bytes 4096 | tf_op jit(solution)/shard_map/all_to_all | solution.py:20
  18.2 1.0 convert_element_type.18
  19.2 4.3 %all-to-all-done.1 = s32[4,1,64]{2,1,0:T(1,128)S(1)} async-done(((s32[4,1,64]{2,1,0:T(1,128)}), s32[4,1,64]{2,1,0:T(1,128)S(1)}, u32[]{:S(2)}, u32[]{:S(2)}) %all-to-all-start.1) | async-done | bytes 1056 | tf_op jit(solution)/shard_map/all_to_all | solution.py:20
  23.5 0.8 broadcast_in_dim.6
  24.3 5.8 %all-to-all-start = ((bf16[4,64,1024]{2,1,0:T(8,128)(2,1)}), bf16[4,64,1024]{2,1,0:T(8,128)(2,1)S(1)}, u32[]{:S(2)}, u32[]{:S(2)}) async-start(bf16[4,64,1024]{2,1,0:T(8,128)(2,1)} %broadcast_in_dim.6), calls=%async_computation | async-start | bytes 1048576 | tf_op jit(solution)/shard_map/all_to_all | solution.py:20
  30.1 0.0 reduce-scatter.3.cloned.1.call-start
  30.1 0.5 broadcast.96
  30.6 0.7 reduce.3
  31.3 0.1 eq.25
  31.4 17.7 %all-to-all-done = bf16[4,64,1024]{2,1,0:T(8,128)(2,1)S(1)} async-done(((bf16[4,64,1024]{2,1,0:T(8,128)(2,1)}), bf16[4,64,1024]{2,1,0:T(8,128)(2,1)S(1)}, u32[]{:S(2)}, u32[]{:S(2)}) %all-to-all-start) | async-done | bytes 524320 | tf_op jit(solution)/shard_map/all_to_all | solution.py:20
  49.1 79.8 %all-gather.2.cloned.1.call-done = bf16[4096,1024]{1,0:T(8,128)(2,1)} async-done(((bf16[64,1024]{1,0:T(8,128)(2,1)}), bf16[4096,1024]{1,0:T(8,128)(2,1)}) %all-gather.2.cloned.1.call-update) | async-done | bytes 8388624 | tf_op jit(solution)/shard_map/all_gather | solution.py:109
  128.9 5.9 %fusion.27 = (f32[256]{0:T(256)S(1)}, f32[256,4096]{1,0:T(8,128)S(1)}) fusion(bf16[256,1024]{1,0:T(8,128)(2,1)S(1)} %bitcast.36, bf16[4096,1024]{1,0:T(8,128)(2,1)} %all-gather.2.cloned.1.call-done), kind=kOutput, calls=%fused_computation.47 | convolution fusion | flops 2149580544 | bytes 13108224 | tf_op jit(solution)/shard_map/dot_general | solution.py:87
  134.8 0.0 copy-start
  134.8 2.0 copy-done
  136.9 1.1 exponential_reduce_fusion
  138.0 11.9 %all_to_all.21 = f32[4,3,256]{2,1,0:T(4,128)S(1)} all-to-all(f32[4,3,256]{2,1,0:T(4,128)S(1)} %broadcast_in_dim.8), channel_id=1, replica_groups=mesh['dp_0'=4,'dp_1'=2,'dp_2'=4,'dp_3'=2,'sub'=4] {'sub'}, dimensions={0} | all-to-all | bytes 24576 | tf_op jit(solution)/shard_map/all_to_all | solution.py:20
  150.0 4.7 %fusion.5 = bf16[4096,256]{0,1:T(8,128)(2,1)} fusion(f32[256,4096]{1,0:T(8,128)} %copy-done, s32[4096]{0:T(1024)S(1)} %fusion.21, f32[256]{0:T(256)S(1)} %bitcast.40, s32[256]{0:T(256)S(1)} %eq.25), kind=kLoop, calls=%fused_computation.10 | loop fusion | flops 6291456 | bytes 6309888 | tf_op jit(solution)/shard_map/convert_element_type | solution.py:120
  154.8 3.3 copy.9
  158.0 2.3 convolution_bitcast_fusion
  160.4 6.0 %copy.10 = f32[2,32,64,1024]{3,2,1,0:T(8,128)} copy(f32[2,32,64,1024]{3,2,0,1:T(8,128)S(1)} %convolution_bitcast_fusion) | data formatting | bytes 33554432 | tf_op jit(solution)/shard_map/transpose | solution.py:74
  166.4 0.0 reduce-scatter.3.cloned.1.call-update
  166.5 0.0 reduce-scatter.5.cloned.1.call-start
  166.5 27.7 %reduce-scatter.3.cloned.1.call-done = f32[32,64,1024]{2,1,0:T(8,128)} async-done(((f32[64,64,1024]{2,1,0:T(8,128)}), f32[32,64,1024]{2,1,0:T(8,128)}) %reduce-scatter.3.cloned.1.call-update) | async-done | bytes 8388624 | tf_op jit(solution)/shard_map/reduce_scatter | solution.py:75
  194.3 0.0 reduce-scatter.5.cloned.1.call-update
  194.3 8.1 %fusion.6 = f32[256,1024]{1,0:T(8,128)} fusion(bf16[4096,1024]{1,0:T(8,128)(2,1)} %all-gather.2.cloned.1.call-done, f32[256,4096]{1,0:T(8,128)} %copy-done, f32[256]{0:T(256)S(1)} %bitcast.41, s32[4096]{0:T(1024)S(1)} %fusion.21, s32[256]{0:T(256)S(1)} %eq.25), kind=kOutput, calls=%fused_computation.13 | convolution fusion | flops 2153775104 | bytes 13649920 | tf_op jit(solution)/shard_map/dot_general | solution.py:121
  202.4 7.4 %all-to-all-start.3 = ((f32[4,64,1024]{2,1,0:T(8,128)}), f32[4,64,1024]{2,1,0:T(8,128)S(1)}, u32[]{:S(2)}, u32[]{:S(2)}) async-start(f32[4,64,1024]{2,1,0:T(8,128)} %bitcast.7), calls=%async_computation.3 | async-start | bytes 2097152 | tf_op jit(solution)/shard_map/all_to_all | solution.py:66
  209.8 0.6 dynamic_slice.3
  210.4 35.8 %all-to-all-done.3 = f32[4,64,1024]{2,1,0:T(8,128)S(1)} async-done(((f32[4,64,1024]{2,1,0:T(8,128)}), f32[4,64,1024]{2,1,0:T(8,128)S(1)}, u32[]{:S(2)}, u32[]{:S(2)}) %all-to-all-start.3) | async-done | bytes 1048608 | tf_op jit(solution)/shard_map/all_to_all | solution.py:66
  246.2 0.8 reduce_sum.29
  247.0 147.6 %reduce-scatter.5.cloned.1.call-done = f32[1,64,1024]{2,1,0:T(8,128)} async-done(((f32[32,64,1024]{2,1,0:T(8,128)}), f32[1,64,1024]{2,1,0:T(8,128)}) %reduce-scatter.5.cloned.1.call-update) | async-done | bytes 262160 | tf_op jit(solution)/shard_map/reduce_scatter | solution.py:76
  (17 shorter events, 0.3 us)
Async XLA Ops:
  7.2 121.8 %all-gather.2.cloned.1.call-start = ((), (), s32[]{:S(2)}) async-start(), calls=%async_computation.6 | async-start | bytes 8519680 | tf_op jit(solution)/shard_map/all_gather | solution.py:109
  10.1 13.4 %all-to-all-start.1 = ((s32[4,1,64]{2,1,0:T(1,128)}), s32[4,1,64]{2,1,0:T(1,128)S(1)}, u32[]{:S(2)}, u32[]{:S(2)}) async-start(s32[4,1,64]{2,1,0:T(1,128)} %broadcast_in_dim.7), calls=%async_computation.1 | async-start | bytes 4096 | tf_op jit(solution)/shard_map/all_to_all | solution.py:20
  24.3 24.8 %all-to-all-start = ((bf16[4,64,1024]{2,1,0:T(8,128)(2,1)}), bf16[4,64,1024]{2,1,0:T(8,128)(2,1)S(1)}, u32[]{:S(2)}, u32[]{:S(2)}) async-start(bf16[4,64,1024]{2,1,0:T(8,128)(2,1)} %broadcast_in_dim.6), calls=%async_computation | async-start | bytes 1048576 | tf_op jit(solution)/shard_map/all_to_all | solution.py:20
  30.1 164.1 %reduce-scatter.3.cloned.1.call-start = ((), (), s32[]{:S(2)}) async-start(), calls=%async_computation.7 | async-start | bytes 25165824 | tf_op jit(solution)/shard_map/reduce_scatter | solution.py:75
  134.8 2.0 copy-start
  166.5 228.1 %reduce-scatter.5.cloned.1.call-start = ((), (), s32[]{:S(2)}) async-start(), calls=%async_computation.8 | async-start | bytes 8650752 | tf_op jit(solution)/shard_map/reduce_scatter | solution.py:76
  202.4 43.8 %all-to-all-start.3 = ((f32[4,64,1024]{2,1,0:T(8,128)}), f32[4,64,1024]{2,1,0:T(8,128)S(1)}, u32[]{:S(2)}, u32[]{:S(2)}) async-start(f32[4,64,1024]{2,1,0:T(8,128)} %bitcast.7), calls=%async_computation.3 | async-start | bytes 2097152 | tf_op jit(solution)/shard_map/all_to_all | solution.py:66
Sparse Core Ops, SparseCore 0:
  10.4 118.4 all-gather.1
  166.6 27.6 reduce-scatter.2
  197.4 197.0 reduce-scatter.4
where the time goes:
time: 402 us; the launch traced here: 401 us
  waiting for transfers between devices  313 us (78%)
  starting transfers between devices  21.4 us (5%)
  matrix products  16.3 us (4%)
  local copies, waits for them, and re-layouts  14.8 us (4%)
  between operations  13.8 us (3%)
  blocking collectives  11.9 us (3%)
  other arithmetic  9.91 us (2%)
    reduce_scatter x1, waiting for transfers between devices, scatter_pairs(): return lax.psum_scatter(blocks, chips, scatter_dimension=0, tiled=True)[0]  148 us
    all_gather x1, waiting for transfers between devices, body(): passage_rows = lax.all_gather(passage_half, DP, axis=0, tiled=True)  79.8 us
    all_to_all x1, waiting for transfers between devices, sum_at_owner(): lax.all_to_all(split_up(value, dim, devices), axis, 0, 0, tiled=True)  35.8 us
    reduce_scatter x1, waiting for transfers between devices, scatter_pairs(): blocks = lax.psum_scatter(blocks, core, scatter_dimension=0, tiled=True)  27.7 us
    all_to_all x2, waiting for transfers between devices, sent_to_all(): lax.all_to_all(jnp.broadcast_to(value[None], (devices, *value.shape)), ax...  22 us
    all_to_all x2, starting transfers between devices, sent_to_all(): lax.all_to_all(jnp.broadcast_to(value[None], (devices, *value.shape)), ax...  13.9 us
    all_to_all x1, blocking collectives, sent_to_all(): lax.all_to_all(jnp.broadcast_to(value[None], (devices, *value.shape)), ax...  11.9 us
    dot_general x1, matrix products, body(): jnp.dot(weights, passage_rows, preferred_element_type=jnp.float32)  8.11 us
  transfers between devices with their start and end apart: 6, of which 6 were waited for; matrix products, arithmetic and copies ran while one was open for 3% of the time, Pallas kernels for 0%

commit v1 on v0

--- a/solution.py
+++ b/solution.py
@@ -106,7 +106,9 @@
     passage_half = passages.astype(jnp.bfloat16)
     query_rows, row_targets = (collect(query_half, "sub", 0), collect(positives, "sub", 0))
     width_cols = row_count * lax.axis_size(DP)
-    passage_rows = lax.all_gather(passage_half, DP, axis=0, tiled=True)
+    passage_rows = jnp.concatenate(
+        lax.all_to_all(jnp.stack([passage_half] * lax.axis_size(DP)), DP, 0, 0), axis=0
+    )
     scores = row_scores(query_rows, passage_rows)
     column = jnp.arange(width_cols, dtype=jnp.int32)
     column_ids = (column // row_count * groups + member) * row_count + column % row_count

time: 402 us -> 434 us (1.080)
  waiting for transfers between devices: 313 us -> 333 us
  starting transfers between devices: 21.4 us -> 29.7 us
    all_to_all x0 -> x1, waiting for transfers between devices: none -> 105 us  [body(): lax.all_to_all(jnp.stack([passage_half] * lax.axis_size(DP)), DP, 0, 0)]
    all_gather x1 -> x0, waiting for transfers between devices: 79.8 us -> none  [body(): passage_rows = lax.all_gather(passage_half, DP, axis=0, tiled=True)]
    all_to_all x0 -> x1, starting transfers between devices: none -> 8.2 us  [body(): lax.all_to_all(jnp.stack([passage_half] * lax.axis_size(DP)), DP, 0, 0)]
    all_to_all x2, waiting for transfers between devices: 22 us -> 17.3 us  [sent_to_all(): lax.all_to_all(jnp.broadcast_to(value[None], (devices, *value.shape)), ax...]
where the time goes in v1:
time: 434 us; the launch traced here: 433 us
  waiting for transfers between devices  333 us (77%)
  starting transfers between devices  29.7 us (7%)
  local copies, waits for them, and re-layouts  19.1 us (4%)
  matrix products  14.9 us (3%)
  between operations  14.1 us (3%)
  other arithmetic  12.6 us (3%)
  blocking collectives  9.95 us (2%)
    reduce_scatter x1, waiting for transfers between devices, scatter_pairs(): return lax.psum_scatter(blocks, chips, scatter_dimension=0, tiled=True)[0]  146 us
    all_to_all x1, waiting for transfers between devices, body(): lax.all_to_all(jnp.stack([passage_half] * lax.axis_size(DP)), DP, 0, 0)  105 us
    all_to_all x1, waiting for transfers between devices, sum_at_owner(): lax.all_to_all(split_up(value, dim, devices), axis, 0, 0, tiled=True)  34.9 us
    reduce_scatter x1, waiting for transfers between devices, scatter_pairs(): blocks = lax.psum_scatter(blocks, core, scatter_dimension=0, tiled=True)  29.5 us
    all_to_all x2, waiting for transfers between devices, sent_to_all(): lax.all_to_all(jnp.broadcast_to(value[None], (devices, *value.shape)), ax...  17.3 us
    all_to_all x2, starting transfers between devices, sent_to_all(): lax.all_to_all(jnp.broadcast_to(value[None], (devices, *value.shape)), ax...  13.9 us
    all_to_all x1, blocking collectives, sent_to_all(): lax.all_to_all(jnp.broadcast_to(value[None], (devices, *value.shape)), ax...  9.95 us
  transfers between devices with their start and end apart: 6, of which 6 were waited for; matrix products, arithmetic and copies ran while one was open for 3% of the time, Pallas kernels for 0%

profile of v1, /device:TPU:64, one launch (start us, length us, event | category | flops | bytes accessed | tf_op | source)
XLA Modules:
  0.0 433.0 jit_solution(215009586957323386)
XLA Ops:
  7.2 1.2 broadcast_in_dim.7
  8.4 8.1 %all-to-all-start.2 = ((s32[4,1,64]{2,1,0:T(1,128)}), s32[4,1,64]{2,1,0:T(1,128)S(1)}, u32[]{:S(2)}, u32[]{:S(2)}) async-start(s32[4,1,64]{2,1,0:T(1,128)} %broadcast_in_dim.7), calls=%async_computation.2 | async-start | bytes 4096 | tf_op jit(solution)/shard_map/all_to_all | solution.py:20
  16.5 1.0 convert_element_type.18
  17.5 4.3 all-to-all-done.2
  21.8 0.8 broadcast_in_dim.6
  22.6 5.8 %all-to-all-start = ((bf16[4,64,1024]{2,1,0:T(8,128)(2,1)}), bf16[4,64,1024]{2,1,0:T(8,128)(2,1)S(1)}, u32[]{:S(2)}, u32[]{:S(2)}) async-start(bf16[4,64,1024]{2,1,0:T(8,128)(2,1)} %broadcast_in_dim.6), calls=%async_computation | async-start | bytes 1048576 | tf_op jit(solution)/shard_map/all_to_all | solution.py:20
  28.4 1.0 convert_element_type.19
  29.4 13.0 %all-to-all-done = bf16[4,64,1024]{2,1,0:T(8,128)(2,1)S(1)} async-done(((bf16[4,64,1024]{2,1,0:T(8,128)(2,1)}), bf16[4,64,1024]{2,1,0:T(8,128)(2,1)S(1)}, u32[]{:S(2)}, u32[]{:S(2)}) %all-to-all-start) | async-done | bytes 524320 | tf_op jit(solution)/shard_map/all_to_all | solution.py:20
  42.4 4.3 stack.2
  46.7 8.2 %all-to-all-start.1 = ((bf16[64,64,1024]{2,1,0:T(8,128)(2,1)}), bf16[64,64,1024]{2,1,0:T(8,128)(2,1)}, u32[]{:S(2)}, u32[]{:S(2)}) async-start(bf16[64,64,1024]{2,1,0:T(8,128)(2,1)} %stack.2), calls=%async_computation.1 | async-start | bytes 16777216 | tf_op jit(solution)/shard_map/all_to_all | solution.py:110
  54.9 0.0 reduce-scatter.3.cloned.1.call-start
  55.0 0.5 broadcast.95
  55.5 0.7 reduce.3
  56.2 0.1 eq.25
  56.2 105.1 %all-to-all-done.1 = bf16[64,64,1024]{2,1,0:T(8,128)(2,1)} async-done(((bf16[64,64,1024]{2,1,0:T(8,128)(2,1)}), bf16[64,64,1024]{2,1,0:T(8,128)(2,1)}, u32[]{:S(2)}, u32[]{:S(2)}) %all-to-all-start.1) | async-done | bytes 8388640 | tf_op jit(solution)/shard_map/all_to_all | solution.py:110
  161.3 5.8 %fusion.20 = (f32[256]{0:T(256)S(1)}, f32[256,4096]{1,0:T(8,128)S(1)}) fusion(bf16[256,1024]{1,0:T(8,128)(2,1)S(1)} %bitcast.40, bf16[4096,1024]{1,0:T(8,128)(2,1)} %bitcast.1), kind=kOutput, calls=%fused_computation.41 | convolution fusion | flops 2149580544 | bytes 13108224 | tf_op jit(solution)/shard_map/dot_general | solution.py:87
  167.2 0.0 copy-start
  167.2 2.0 copy-done
  169.2 1.1 exponential_reduce_fusion
  170.3 9.9 %all_to_all.26 = f32[4,3,256]{2,1,0:T(4,128)S(1)} all-to-all(f32[4,3,256]{2,1,0:T(4,128)S(1)} %broadcast_in_dim.8), channel_id=1, replica_groups=mesh['dp_0'=4,'dp_1'=2,'dp_2'=4,'dp_3'=2,'sub'=4] {'sub'}, dimensions={0} | all-to-all | bytes 24576 | tf_op jit(solution)/shard_map/all_to_all | solution.py:20
  180.5 4.7 %fusion.5 = bf16[4096,256]{0,1:T(8,128)(2,1)} fusion(f32[256,4096]{1,0:T(8,128)} %copy-done, s32[4096]{0:T(1024)S(1)} %fusion.15, f32[256]{0:T(256)S(1)} %bitcast.43, s32[256]{0:T(256)S(1)} %eq.25), kind=kLoop, calls=%fused_computation.10 | loop fusion | flops 6291456 | bytes 6309888 | tf_op jit(solution)/shard_map/convert_element_type | solution.py:122
  185.2 3.3 copy.9
  188.4 2.3 convolution_bitcast_fusion
  190.8 6.0 %copy.10 = f32[2,32,64,1024]{3,2,1,0:T(8,128)} copy(f32[2,32,64,1024]{3,2,0,1:T(8,128)S(1)} %convolution_bitcast_fusion) | data formatting | bytes 33554432 | tf_op jit(solution)/shard_map/transpose | solution.py:74
  196.8 0.0 reduce-scatter.3.cloned.1.call-update
  196.9 0.2 reduce-scatter.5.cloned.1.call-start
  197.1 29.5 %reduce-scatter.3.cloned.1.call-done = f32[32,64,1024]{2,1,0:T(8,128)} async-done(((f32[64,64,1024]{2,1,0:T(8,128)}), f32[32,64,1024]{2,1,0:T(8,128)}) %reduce-scatter.3.cloned.1.call-update) | async-done | bytes 8388624 | tf_op jit(solution)/shard_map/reduce_scatter | solution.py:75
  226.6 0.0 reduce-scatter.5.cloned.1.call-update
  226.6 3.3 fusion.3
  229.9 6.7 %fusion.21 = f32[4,64,1024]{2,1,0:T(8,128)} fusion(bf16[4,64,4096]{2,1,0:T(8,128)(2,1)S(1)} %bitcast.42, bf16[4096,1024,1]{1,0,2:T(8,128)(2,1)} %bitcast.9), kind=kOutput, calls=%fused_computation.42 | convolution fusion | flops 2147483648 | bytes 11534336 | tf_op jit(solution)/shard_map/dot_general | solution.py:123
  236.6 7.4 %all-to-all-start.4 = ((f32[4,64,1024]{2,1,0:T(8,128)}), f32[4,64,1024]{2,1,0:T(8,128)S(1)}, u32[]{:S(2)}, u32[]{:S(2)}) async-start(f32[4,64,1024]{2,1,0:T(8,128)} %fusion.21), calls=%async_computation.4 | async-start | bytes 2097152 | tf_op jit(solution)/shard_map/all_to_all | solution.py:66
  244.0 0.6 dynamic_slice.3
  244.6 34.9 %all-to-all-done.4 = f32[4,64,1024]{2,1,0:T(8,128)S(1)} async-done(((f32[4,64,1024]{2,1,0:T(8,128)}), f32[4,64,1024]{2,1,0:T(8,128)S(1)}, u32[]{:S(2)}, u32[]{:S(2)}) %all-to-all-start.4) | async-done | bytes 1048608 | tf_op jit(solution)/shard_map/all_to_all | solution.py:66
  279.5 0.8 reduce_sum.29
  280.3 145.8 %reduce-scatter.5.cloned.1.call-done = f32[1,64,1024]{2,1,0:T(8,128)} async-done(((f32[32,64,1024]{2,1,0:T(8,128)}), f32[1,64,1024]{2,1,0:T(8,128)}) %reduce-scatter.5.cloned.1.call-update) | async-done | bytes 262160 | tf_op jit(solution)/shard_map/reduce_scatter | solution.py:76
  (17 shorter events, 0.3 us)
Async XLA Ops:
  8.4 13.4 %all-to-all-start.2 = ((s32[4,1,64]{2,1,0:T(1,128)}), s32[4,1,64]{2,1,0:T(1,128)S(1)}, u32[]{:S(2)}, u32[]{:S(2)}) async-start(s32[4,1,64]{2,1,0:T(1,128)} %broadcast_in_dim.7), calls=%async_computation.2 | async-start | bytes 4096 | tf_op jit(solution)/shard_map/all_to_all | solution.py:20
  22.6 19.8 %all-to-all-start = ((bf16[4,64,1024]{2,1,0:T(8,128)(2,1)}), bf16[4,64,1024]{2,1,0:T(8,128)(2,1)S(1)}, u32[]{:S(2)}, u32[]{:S(2)}) async-start(bf16[4,64,1024]{2,1,0:T(8,128)(2,1)} %broadcast_in_dim.6), calls=%async_computation | async-start | bytes 1048576 | tf_op jit(solution)/shard_map/all_to_all | solution.py:20
  46.7 114.6 %all-to-all-start.1 = ((bf16[64,64,1024]{2,1,0:T(8,128)(2,1)}), bf16[64,64,1024]{2,1,0:T(8,128)(2,1)}, u32[]{:S(2)}, u32[]{:S(2)}) async-start(bf16[64,64,1024]{2,1,0:T(8,128)(2,1)} %stack.2), calls=%async_computation.1 | async-start | bytes 16777216 | tf_op jit(solution)/shard_map/all_to_all | solution.py:110
  54.9 171.6 %reduce-scatter.3.cloned.1.call-start = ((), (), s32[]{:S(2)}) async-start(), calls=%async_computation.7 | async-start | bytes 25165824 | tf_op jit(solution)/shard_map/reduce_scatter | solution.py:75
  167.2 2.1 copy-start
  196.9 229.3 %reduce-scatter.5.cloned.1.call-start = ((), (), s32[]{:S(2)}) async-start(), calls=%async_computation.8 | async-start | bytes 8650752 | tf_op jit(solution)/shard_map/reduce_scatter | solution.py:76
  236.6 42.9 %all-to-all-start.4 = ((f32[4,64,1024]{2,1,0:T(8,128)}), f32[4,64,1024]{2,1,0:T(8,128)S(1)}, u32[]{:S(2)}, u32[]{:S(2)}) async-start(f32[4,64,1024]{2,1,0:T(8,128)} %fusion.21), calls=%async_computation.4 | async-start | bytes 2097152 | tf_op jit(solution)/shard_map/all_to_all | solution.py:66
Sparse Core Ops, SparseCore 0:
  197.0 29.5 reduce-scatter.2
  229.7 196.4 reduce-scatter.4
